TPU v7x, 32 devices: a whole 2x2x4 slice. The times are simulated.
32 devices in a mesh: row: 8 (over y, x, core), col: 4 (over z).
Axes of the slice: x: 2, y: 2, z: 4, core: 2. Of those that a mesh axis runs over, the one named last changes fastest.
Arguments:
- positions: float32 [3, 16384], P(None, ('row', 'col')), may hold values from -6 to 6
- velocities: float32 [3, 16384], P(None, ('row', 'col')), may hold values from -6 to 6
- accels: float32 [3, 16384], P(None, ('row', 'col')), may hold values from -0.75 to 0.75
- jerks: float32 [3, 16384], P(None, ('row', 'col')), may hold values from -1.5 to 1.5
- masses: float32 [16384], P(('row', 'col')), may hold values from 0.3 to 3
- elapsed: float32 [16384], P(('row', 'col')), may hold values from 0.05 to 0.5
- active_star: int32 [1024], replicated, may hold values from 0 to 16383, as said below
Outputs:
- new_positions: float32 [3, 16384], P(None, ('row', 'col'))
- new_velocities: float32 [3, 16384], P(None, ('row', 'col'))
- new_accels: float32 [3, 16384], P(None, ('row', 'col'))
- new_jerks: float32 [3, 16384], P(None, ('row', 'col'))
Inputs may be any that keep to these rules, and one draw needn't show every extreme that they name: `active_star`: the 1024 ids are distinct. Star g is owned by device g // 512, devices counted with row slowest and col fastest. In each aligned block of 128 entries (one group of targets), at most 48 entries name stars whose owning device has the same col index, and in every block some col index has exactly 48.
All inputs are finite; a program needn't handle non-finite values.
Results may differ from a plain program's by a relative error of at most 0.0003.
Values sent between devices are 32-bit elements; how exact they have to be, the bound alone decides.
No kernel may reach another device: no remote copies, remote signals or barrier semaphores. Data moves between devices by JAX's collectives and lax.ppermute only.
A program may use at most 64 MiB of HBM per device.

v0:
```python
import math
import jax
import jax.numpy as jnp
from jax import lax
from jax.sharding import PartitionSpec as P

softening = 0.001


def predict(positions, velocities, accels, jerks, elapsed):
    timestep = elapsed[None, :]
    moved_pos = positions + timestep * (
        velocities + timestep * (0.5 * accels + timestep * jerks / 6.0)
    )
    moved_vel = velocities + timestep * (accels + 0.5 * timestep * jerks)
    return (moved_pos, moved_vel)


def correct(old_pos, old_vel, old_acc, old_jerk, new_acc, new_jerk, timestep):
    halfstep = 0.5 * timestep
    twelfth = timestep * timestep / 12.0
    new_vel = old_vel + halfstep * (old_acc + new_acc) + twelfth * (old_jerk - new_jerk)
    new_pos = old_pos + halfstep * (old_vel + new_vel) + twelfth * (old_acc - new_acc)
    return (new_pos, new_vel)


def pair_sums(targets, sources, ceiling):
    jcount = sources.shape[1]
    blk_width = math.gcd(jcount, ceiling)
    jpieces = jnp.transpose(sources.reshape(7, jcount // blk_width, blk_width), (1, 0, 2))

    def advance(running, jpiece):
        separation = jpiece[0:3, None, :] - targets[0:3, :, None]
        rel_velocity = jpiece[3:6, None, :] - targets[3:6, :, None]
        radius_sq = jnp.sum(separation * separation, axis=0) + softening
        inverse = lax.rsqrt(radius_sq)
        weight = jpiece[6][None, :] * inverse * inverse * inverse
        closing = 3.0 * jnp.sum(separation * rel_velocity, axis=0) / radius_sq
        accel_sum = jnp.sum(weight[None] * separation, axis=2)
        change = jnp.sum(weight[None] * (rel_velocity - closing[None] * separation), axis=2)
        return (running + jnp.concatenate([accel_sum, change], axis=0), None)

    initial = jnp.zeros((6, targets.shape[1]), jnp.float32)
    summed, unused = lax.scan(advance, initial, jpieces)
    return summed


def on_device(positions, velocities, accels, jerks, masses, elapsed, active_star):
    star_dev = positions.shape[1]
    row_count = lax.axis_size("row")
    col_count = lax.axis_size("col")
    row_index = lax.axis_index("row")
    col_index = lax.axis_index("col")
    device_id = row_index * col_count + col_index
    active_count = active_star.shape[0]
    group_size = active_count // row_count
    scale = 1.0 / (star_dev * row_count * col_count)
    highest = lax.Precision.HIGHEST
    moved_pos, moved_vel = predict(positions, velocities, accels, jerks, elapsed)
    sources = jnp.concatenate([moved_pos, moved_vel, masses[None, :]], axis=0)
    group_ids = lax.dynamic_slice_in_dim(active_star, row_index * group_size, group_size)
    in_column = group_ids // star_dev % col_count == col_index
    column_block = lax.all_gather(sources, "row", axis=1, tiled=True)
    position_in = group_ids // star_dev // col_count * star_dev + group_ids % star_dev
    slot_rows = lax.broadcasted_iota(jnp.int32, (column_block.shape[1], group_size), 0)
    picker = ((slot_rows == position_in[None, :]) & in_column[None, :]).astype(jnp.float32)
    own_part = jnp.dot(
        column_block[0:6], picker, precision=highest, preferred_element_type=jnp.float32
    )
    targets = lax.psum(own_part, "col")
    partial_sums = pair_sums(targets, column_block, 512)
    forces = lax.psum(partial_sums, "col") * scale
    every_force = lax.all_gather(forces, "row", axis=1, tiled=True)
    slot_cols = lax.broadcasted_iota(jnp.int32, (active_count, star_dev), 1)
    mine = (active_star // star_dev == device_id)[:, None]
    placer = (mine & ((active_star % star_dev)[:, None] == slot_cols)).astype(jnp.float32)
    landed = jnp.dot(every_force, placer, precision=highest, preferred_element_type=jnp.float32)
    flags = jnp.sum(placer, axis=0)
    active = (flags > 0.5)[None, :]
    new_acc = landed[0:3]
    new_jerk = landed[3:6]
    new_pos, new_vel = correct(
        positions, velocities, accels, jerks, new_acc, new_jerk, elapsed[None, :]
    )
    return (
        jnp.where(active, new_pos, positions),
        jnp.where(active, new_vel, velocities),
        jnp.where(active, new_acc, accels),
        jnp.where(active, new_jerk, jerks),
    )


def solution(mesh):
    placed = (
        P(None, ("row", "col")),
        P(None, ("row", "col")),
        P(None, ("row", "col")),
        P(None, ("row", "col")),
        P(("row", "col")),
        P(("row", "col")),
        P(),
    )
    return jax.shard_map(
        on_device,
        mesh=mesh,
        in_specs=placed,
        out_specs=(
            P(None, ("row", "col")),
            P(None, ("row", "col")),
            P(None, ("row", "col")),
            P(None, ("row", "col")),
        ),
        check_vma=False,
    )
```

profile of v0, /device:TPU:0, one launch (start us, length us, event | category | flops | bytes accessed | tf_op | source)
XLA Modules:
  0.0 54.1 jit_solution(8628084013568798140)
XLA Ops:
  0.6 0.8 %fusion.20 = (pred[128]{0:T(512)(128)(4,1)S(1)}, s32[128]{0:T(128)S(1)}) fusion(s32[]{:T(128)S(6)} %axis_index.25, s32[1024]{0:T(1024)} %param.15, s32[]{:T(128)S(6)} %select_n.49), kind=kLoop, calls=%fused_computation.60 | loop fusion | flops 3456 | bytes 1160 | tf_op jit(solution)/shard_map/eq | solution.py:62
  1.4 0.8 %fusion.19 = s32[128]{0:T(128)S(1)} fusion(s32[128]{0:T(128)S(1)} %get-tuple-element.55, s32[1024]{0:T(1024)} %param.15, s32[]{:T(128)S(6)} %select_n.49), kind=kLoop, calls=%fused_computation.59 | loop fusion | flops 3584 | bytes 1540 | tf_op jit(solution)/shard_map/add | solution.py:64
  2.2 0.7 %multiply_multiply_fusion.1 = (f32[512]{0:T(512)S(1)}, f32[512]{0:T(512)S(1)}) fusion(f32[512]{0:T(512)} %param.14), kind=kLoop, calls=%fused_computation.45 | loop fusion | flops 1536 | bytes 6144 | tf_op jit(solution)/shard_map/div | solution.py:21
  2.9 0.8 %multiply_add_fusion.2 = (f32[3,512]{1,0:T(4,128)S(1)}, f32[3,512]{1,0:T(4,128)S(1)}) fusion(f32[3,512]{1,0:T(4,128)} %param.9, f32[3,512]{1,0:T(4,128)} %param.10, f32[3,512]{1,0:T(4,128)} %param.12, f32[3,512]{1,0:T(4,128)} %param.11, f32[512]{0:T(512)} %param.14, f32[512]{0:T(512)S(1)} %get-tuple-element.69), kind=kLoop, calls=%fused_computation.32 | loop fusion | flops 18432 | bytes 40960 | tf_op jit(solution)/shard_map/add | solution.py:12
  3.6 0.7 %pad_maximum_fusion = f32[7,512]{1,0:T(8,128)S(1)} fusion(f32[1,512]{1,0:T(1,128)} %bitcast.16, f32[3,512]{1,0:T(4,128)S(1)} %get-tuple-element.65, f32[3,512]{1,0:T(4,128)S(1)} %get-tuple-element.64), kind=kLoop, calls=%fused_computation.28 | loop fusion | flops 7168 | bytes 28672 | tf_op jit(solution)/shard_map/concatenate | solution.py:60
  4.3 10.7 %all_gather.6 = f32[7,4096]{1,0:T(8,128)S(1)} all-gather(f32[7,512]{1,0:T(8,128)S(1)} %pad_maximum_fusion), channel_id=1, replica_groups=mesh['row'=8,'col'=4] {'row'}, dimensions={1}, use_global_device_ids=true | all-gather | bytes 129024 | tf_op jit(solution)/shard_map/all_gather | solution.py:63
  15.0 0.8 %fusion.9 = f32[6,128]{1,0:T(8,128)S(1)} fusion(s32[128]{0:T(128)S(1)} %fusion.19, pred[128]{0:T(512)(128)(4,1)S(1)} %get-tuple-element.54, f32[7,4096]{1,0:T(8,128)S(1)} %all_gather.6), kind=kOutput, calls=%fused_computation.22 | convolution fusion | flops 38797312 | bytes 118400 | tf_op jit(solution)/shard_map/dot_general | solution.py:67
  15.9 12.0 %psum.14 = f32[6,128]{1,0:T(8,128)S(1)} all-reduce(f32[6,128]{1,0:T(8,128)S(1)} %fusion.9), channel_id=1, replica_groups=mesh['row'=8,'col'=4] {'col'}, use_global_device_ids=true, to_apply=%region_1.2 | all-reduce | flops 768 | bytes 6144 | tf_op jit(solution)/shard_map/psum | solution.py:70
  27.8 6.4 %while.11 = (s32[]{:T(128)}, f32[6,128]{1,0:T(8,128)S(1)}, f32[8,7,512]{2,1,0:T(8,128)S(1)}, f32[6,128]{1,0:T(8,128)S(1)}, s32[]{:T(128)}, /*index=5*/s32[]{:T(128)}, s32[]{}, s32[]{}) while((s32[]{:T(128)}, f32[6,128]{1,0:T(8,128)S(1)}, f32[8,7,512]{2,1,0:T(8,128)S(1)}, f32[6,128]{1,0:T(8,128)S(1)}, s32[]{:T(128)}, ...), condition=%wide.region_7.8_spmd.clone, body=%wide.region_2.0_spmd.clone.sunk | while | flops 3016197 | bytes 2177159 | solution.py:44
  27.9 0.2 fusion.27
  28.1 0.1 multiply_divide_fusion.2
  28.2 0.4 fusion.28
  28.7 0.2 fusion.27
  29.0 0.4 fusion.28
  29.5 0.2 fusion.27
  29.8 0.4 fusion.28
  30.3 0.2 fusion.27
  30.5 0.1 multiply_divide_fusion.2
  30.6 0.4 fusion.28
  31.1 0.2 fusion.27
  31.4 0.4 fusion.28
  31.9 0.2 fusion.27
  32.2 0.4 fusion.28
  32.7 0.2 fusion.27
  33.0 0.4 fusion.28
  33.5 0.2 fusion.27
  33.8 0.4 fusion.28
  34.2 8.4 %psum.15 = f32[6,128]{1,0:T(8,128)S(1)} all-reduce(f32[6,128]{1,0:T(8,128)S(1)} %get-tuple-element.26), channel_id=1, replica_groups=mesh['row'=8,'col'=4] {'col'}, use_global_device_ids=true, to_apply=%region_8.9 | all-reduce | flops 768 | bytes 6144 | tf_op jit(solution)/shard_map/psum | solution.py:72
  42.6 9.1 %all_gather.7 = f32[6,1024]{1,0:T(8,128)S(1)} all-gather(f32[6,128]{1,0:T(8,128)S(1)} %broadcast_multiply_fusion), channel_id=1, replica_groups=mesh['row'=8,'col'=4] {'row'}, dimensions={1}, use_global_device_ids=true | all-gather | bytes 27648 | tf_op jit(solution)/shard_map/all_gather | solution.py:73
  51.8 0.9 %fusion.6 = f32[6,512]{1,0:T(8,128)S(1)} fusion(f32[6,1024]{1,0:T(8,128)S(1)} %all_gather.7, s32[1024]{0:T(1024)S(1)} %add_select_fusion.1, pred[1024]{0:T(1024)(128)(4,1)S(1)} %fusion.16), kind=kOutput, calls=%fused_computation.20 | convolution fusion | flops 38797312 | bytes 41984 | tf_op jit(solution)/shard_map/dot_general | solution.py:77
  52.6 0.8 %convert_reduce_fusion = f32[512]{0:T(512)S(1)} fusion(s32[1024]{0:T(1024)S(1)} %add_select_fusion.1, pred[1024]{0:T(1024)(128)(4,1)S(1)} %fusion.16), kind=kLoop, calls=%fused_computation.17 | loop fusion | flops 2096640 | bytes 7168 | tf_op jit(solution)/shard_map/reduce_sum | solution.py:78
  53.5 0.6 %broadcast_select_fusion = (f32[3,512]{1,0:T(4,128)}, f32[3,512]{1,0:T(4,128)}, f32[3,512]{1,0:T(4,128)}, f32[3,512]{1,0:T(4,128)}) fusion(f32[3,512]{1,0:T(4,128)S(1)} %copy-done, pred[512]{0:T(512)(128)(4,1)S(1)} %broadcast_compare_fusion, f32[3,512]{1,0:T(4,128)S(1)} %copy-done.1, f32[6,512]{1,0:T(8,128)S(1)} %fusion.6, f32[512]{0:T(512)S(1)} %get-tuple-element.68, ...), kind=kLoop, calls=%fused_computation.43 | loop fusion | flops 24576 | bytes 66048 | tf_op jit(solution)/shard_map/jit(_where)/select_n | solution.py:87
  (53 shorter events, 0.9 us)
Async XLA Ops:
  27.8 23.9 %copy-start.4 = (s32[1024]{0:T(1024)S(1)}, s32[1024]{0:T(1024)}, u32[]{:S(2)}) copy-start(s32[1024]{0:T(1024)} %param.15) | copy-start | bytes 12292
  51.7 1.7 %copy-start = (f32[3,512]{1,0:T(4,128)S(1)}, f32[3,512]{1,0:T(4,128)}, u32[]{:S(2)}) copy-start(f32[3,512]{1,0:T(4,128)} %param.10) | copy-start | bytes 18436
  51.7 1.7 %copy-start.1 = (f32[3,512]{1,0:T(4,128)S(1)}, f32[3,512]{1,0:T(4,128)}, u32[]{:S(2)}) copy-start(f32[3,512]{1,0:T(4,128)} %param.12) | copy-start | bytes 18436
  51.8 1.7 %copy-start.2 = (f32[3,512]{1,0:T(4,128)S(1)}, f32[3,512]{1,0:T(4,128)}, u32[]{:S(2)}) copy-start(f32[3,512]{1,0:T(4,128)} %param.9) | copy-start | bytes 18436
  51.8 1.7 %copy-start.3 = (f32[3,512]{1,0:T(4,128)S(1)}, f32[3,512]{1,0:T(4,128)}, u32[]{:S(2)}) copy-start(f32[3,512]{1,0:T(4,128)} %param.11) | copy-start | bytes 18436
where the time goes:
time: 54.5 us; the launch traced here: 54.1 us
  blocking collectives  40.1 us (74%)
  other arithmetic  10.8 us (20%)
  matrix products  1.7 us (3%)
  between operations  0.73 us (1%)
    psum x1, blocking collectives, on_device(): targets = lax.psum(own_part, 'col')  12 us
    all_gather x1, blocking collectives, on_device(): column_block = lax.all_gather(sources, 'row', axis=1, tiled=True)  10.7 us
    all_gather x1, blocking collectives, on_device(): every_force = lax.all_gather(forces, 'row', axis=1, tiled=True)  9.08 us
    psum x1, blocking collectives, on_device(): forces = lax.psum(partial_sums, 'col') * scale  8.38 us
    reduce_sum x8, other arithmetic, advance(): accel_sum = jnp.sum(weight[None] * separation, axis=2)  3.21 us
    reduce_sum x8, other arithmetic, advance(): radius_sq = jnp.sum(separation * separation, axis=0) + softening  1.73 us

commit v1 on v0

--- a/solution.py
+++ b/solution.py
@@ -69,7 +69,7 @@
     )
     targets = lax.psum(own_part, "col")
     partial_sums = pair_sums(targets, column_block, 512)
-    forces = lax.psum(partial_sums, "col") * scale
+    forces = jnp.sum(lax.all_gather(partial_sums, "col"), axis=0) * scale
     every_force = lax.all_gather(forces, "row", axis=1, tiled=True)
     slot_cols = lax.broadcasted_iota(jnp.int32, (active_count, star_dev), 1)
     mine = (active_star // star_dev == device_id)[:, None]

time: 54.5 us -> 59.3 us (1.088)
  blocking collectives: 40.1 us -> 45 us
    all_gather x0 -> x1, blocking collectives: none -> 13.2 us  [on_device(): forces = jnp.sum(lax.all_gather(partial_sums, 'col'), axis=0) * scale]
    psum x1 -> x0, blocking collectives: 8.38 us -> none  [on_device(): forces = lax.psum(partial_sums, 'col') * scale]
where the time goes in v1:
time: 59.3 us; the launch traced here: 58.9 us
  blocking collectives  45 us (76%)
  other arithmetic  10.8 us (18%)
  matrix products  1.7 us (3%)
  between operations  0.74 us (1%)
    all_gather x1, blocking collectives, on_device(): forces = jnp.sum(lax.all_gather(partial_sums, 'col'), axis=0) * scale  13.2 us
    psum x1, blocking collectives, on_device(): targets = lax.psum(own_part, 'col')  12 us
    all_gather x1, blocking collectives, on_device(): column_block = lax.all_gather(sources, 'row', axis=1, tiled=True)  10.7 us
    all_gather x1, blocking collectives, on_device(): every_force = lax.all_gather(forces, 'row', axis=1, tiled=True)  9.09 us
    reduce_sum x8, other arithmetic, advance(): accel_sum = jnp.sum(weight[None] * separation, axis=2)  3.21 us
    reduce_sum x8, other arithmetic, advance(): radius_sq = jnp.sum(separation * separation, axis=0) + softening  1.73 us

profile of v1, /device:TPU:0, one launch (start us, length us, event | category | flops | bytes accessed | tf_op | source)
XLA Modules:
  0.0 58.9 jit_solution(15839885204301427459)
XLA Ops:
  0.6 0.8 %fusion.20 = (pred[128]{0:T(512)(128)(4,1)S(1)}, s32[128]{0:T(128)S(1)}) fusion(s32[]{:T(128)S(6)} %axis_index.25, s32[1024]{0:T(1024)} %param.15, s32[]{:T(128)S(6)} %select_n.49), kind=kLoop, calls=%fused_computation.60 | loop fusion | flops 3456 | bytes 1160 | tf_op jit(solution)/shard_map/eq | solution.py:62
  1.4 0.8 %fusion.19 = s32[128]{0:T(128)S(1)} fusion(s32[128]{0:T(128)S(1)} %get-tuple-element.55, s32[1024]{0:T(1024)} %param.15, s32[]{:T(128)S(6)} %select_n.49), kind=kLoop, calls=%fused_computation.59 | loop fusion | flops 3584 | bytes 1540 | tf_op jit(solution)/shard_map/add | solution.py:64
  2.2 0.7 %multiply_multiply_fusion.1 = (f32[512]{0:T(512)S(1)}, f32[512]{0:T(512)S(1)}) fusion(f32[512]{0:T(512)} %param.14), kind=kLoop, calls=%fused_computation.45 | loop fusion | flops 1536 | bytes 6144 | tf_op jit(solution)/shard_map/div | solution.py:21
  2.9 0.8 %multiply_add_fusion.2 = (f32[3,512]{1,0:T(4,128)S(1)}, f32[3,512]{1,0:T(4,128)S(1)}) fusion(f32[3,512]{1,0:T(4,128)} %param.9, f32[3,512]{1,0:T(4,128)} %param.10, f32[3,512]{1,0:T(4,128)} %param.12, f32[3,512]{1,0:T(4,128)} %param.11, f32[512]{0:T(512)} %param.14, f32[512]{0:T(512)S(1)} %get-tuple-element.69), kind=kLoop, calls=%fused_computation.32 | loop fusion | flops 18432 | bytes 40960 | tf_op jit(solution)/shard_map/add | solution.py:12
  3.6 0.7 %pad_maximum_fusion = f32[7,512]{1,0:T(8,128)S(1)} fusion(f32[1,512]{1,0:T(1,128)} %bitcast.18, f32[3,512]{1,0:T(4,128)S(1)} %get-tuple-element.65, f32[3,512]{1,0:T(4,128)S(1)} %get-tuple-element.64), kind=kLoop, calls=%fused_computation.28 | loop fusion | flops 7168 | bytes 28672 | tf_op jit(solution)/shard_map/concatenate | solution.py:60
  4.3 10.7 %all_gather.12 = f32[7,4096]{1,0:T(8,128)S(1)} all-gather(f32[7,512]{1,0:T(8,128)S(1)} %pad_maximum_fusion), channel_id=1, replica_groups=mesh['row'=8,'col'=4] {'row'}, dimensions={1}, use_global_device_ids=true | all-gather | bytes 129024 | tf_op jit(solution)/shard_map/all_gather | solution.py:63
  15.0 0.8 %fusion.9 = f32[6,128]{1,0:T(8,128)S(1)} fusion(s32[128]{0:T(128)S(1)} %fusion.19, pred[128]{0:T(512)(128)(4,1)S(1)} %get-tuple-element.54, f32[7,4096]{1,0:T(8,128)S(1)} %all_gather.12), kind=kOutput, calls=%fused_computation.22 | convolution fusion | flops 38797312 | bytes 118400 | tf_op jit(solution)/shard_map/dot_general | solution.py:67
  15.9 12.0 %psum.7 = f32[6,128]{1,0:T(8,128)S(1)} all-reduce(f32[6,128]{1,0:T(8,128)S(1)} %fusion.9), channel_id=1, replica_groups=mesh['row'=8,'col'=4] {'col'}, use_global_device_ids=true, to_apply=%region_1.2 | all-reduce | flops 768 | bytes 6144 | tf_op jit(solution)/shard_map/psum | solution.py:70
  27.8 6.4 %while.11 = (s32[]{:T(128)}, f32[6,128]{1,0:T(8,128)S(1)}, f32[8,7,512]{2,1,0:T(8,128)S(1)}, f32[6,128]{1,0:T(8,128)S(1)}, s32[]{:T(128)}, /*index=5*/s32[]{:T(128)}, s32[]{}, s32[]{}) while((s32[]{:T(128)}, f32[6,128]{1,0:T(8,128)S(1)}, f32[8,7,512]{2,1,0:T(8,128)S(1)}, f32[6,128]{1,0:T(8,128)S(1)}, s32[]{:T(128)}, ...), condition=%wide.region_7.8_spmd.clone, body=%wide.region_2.0_spmd.clone.sunk | while | flops 3016197 | bytes 2177159 | solution.py:44
  27.9 0.2 fusion.27
  28.1 0.1 multiply_divide_fusion.2
  28.2 0.4 fusion.28
  28.7 0.2 fusion.27
  29.0 0.4 fusion.28
  29.5 0.2 fusion.27
  29.8 0.4 fusion.28
  30.3 0.2 fusion.27
  30.5 0.1 multiply_divide_fusion.2
  30.6 0.4 fusion.28
  31.1 0.2 fusion.27
  31.4 0.4 fusion.28
  31.9 0.2 fusion.27
  32.2 0.4 fusion.28
  32.7 0.2 fusion.27
  33.0 0.4 fusion.28
  33.5 0.2 fusion.27
  33.8 0.4 fusion.28
  34.2 13.2 %all-gather.1 = f32[4,6,128]{2,1,0:T(8,128)S(1)} all-gather(f32[1,6,128]{2,1,0:T(8,128)S(1)} %bitcast.17), channel_id=2, replica_groups=mesh['row'=8,'col'=4] {'col'}, dimensions={0}, use_global_device_ids=true | all-gather | bytes 15360 | tf_op jit(solution)/shard_map/all_gather | solution.py:72
  47.5 9.1 %all_gather.15 = f32[6,1024]{1,0:T(8,128)S(1)} all-gather(f32[6,128]{1,0:T(8,128)S(1)} %broadcast_multiply_fusion), channel_id=1, replica_groups=mesh['row'=8,'col'=4] {'row'}, dimensions={1}, use_global_device_ids=true | all-gather | bytes 27648 | tf_op jit(solution)/shard_map/all_gather | solution.py:73
  56.6 0.9 %fusion.6 = f32[6,512]{1,0:T(8,128)S(1)} fusion(f32[6,1024]{1,0:T(8,128)S(1)} %all_gather.15, s32[1024]{0:T(1024)S(1)} %add_select_fusion.1, pred[1024]{0:T(1024)(128)(4,1)S(1)} %fusion.16), kind=kOutput, calls=%fused_computation.20 | convolution fusion | flops 38797312 | bytes 41984 | tf_op jit(solution)/shard_map/dot_general | solution.py:77
  57.5 0.8 %convert_reduce_fusion = f32[512]{0:T(512)S(1)} fusion(s32[1024]{0:T(1024)S(1)} %add_select_fusion.1, pred[1024]{0:T(1024)(128)(4,1)S(1)} %fusion.16), kind=kLoop, calls=%fused_computation.17 | loop fusion | flops 2096640 | bytes 7168 | tf_op jit(solution)/shard_map/reduce_sum | solution.py:78
  58.3 0.6 %broadcast_select_fusion = (f32[3,512]{1,0:T(4,128)}, f32[3,512]{1,0:T(4,128)}, f32[3,512]{1,0:T(4,128)}, f32[3,512]{1,0:T(4,128)}) fusion(f32[3,512]{1,0:T(4,128)S(1)} %copy-done, pred[512]{0:T(512)(128)(4,1)S(1)} %broadcast_compare_fusion, f32[3,512]{1,0:T(4,128)S(1)} %copy-done.1, f32[6,512]{1,0:T(8,128)S(1)} %fusion.6, f32[512]{0:T(512)S(1)} %get-tuple-element.68, ...), kind=kLoop, calls=%fused_computation.43 | loop fusion | flops 24576 | bytes 66048 | tf_op jit(solution)/shard_map/jit(_where)/select_n | solution.py:87
  (54 shorter events, 0.9 us)
Async XLA Ops:
  27.8 28.7 %copy-start.4 = (s32[1024]{0:T(1024)S(1)}, s32[1024]{0:T(1024)}, u32[]{:S(2)}) copy-start(s32[1024]{0:T(1024)} %param.15) | copy-start | bytes 12292
  56.6 1.7 %copy-start = (f32[3,512]{1,0:T(4,128)S(1)}, f32[3,512]{1,0:T(4,128)}, u32[]{:S(2)}) copy-start(f32[3,512]{1,0:T(4,128)} %param.10) | copy-start | bytes 18436
  56.6 1.7 %copy-start.1 = (f32[3,512]{1,0:T(4,128)S(1)}, f32[3,512]{1,0:T(4,128)}, u32[]{:S(2)}) copy-start(f32[3,512]{1,0:T(4,128)} %param.12) | copy-start | bytes 18436
  56.6 1.7 %copy-start.2 = (f32[3,512]{1,0:T(4,128)S(1)}, f32[3,512]{1,0:T(4,128)}, u32[]{:S(2)}) copy-start(f32[3,512]{1,0:T(4,128)} %param.9) | copy-start | bytes 18436
  56.6 1.7 %copy-start.3 = (f32[3,512]{1,0:T(4,128)S(1)}, f32[3,512]{1,0:T(4,128)}, u32[]{:S(2)}) copy-start(f32[3,512]{1,0:T(4,128)} %param.11) | copy-start | bytes 18436
